TPU v7x, 32 devices: a whole 2x2x4 slice. The times are simulated.
32 devices in a mesh: gx: 8 (over z, x), gy: 4 (over y, core).
Axes of the slice: x: 2, y: 2, z: 4, core: 2. Of those that a mesh axis runs over, the one named last changes fastest.
Arguments:
- velocity: float32 [3, 8192, 512], P(None, ('gx', 'gy')), may hold values from -6 to 6
- positions: float32 [3, 1024, 256], P(None, ('gx', 'gy')), may hold values from -6 to 6
- stiff_h: float32 [1024, 256], P(('gx', 'gy')), may hold values from 0.1 to 1
- stiff_v: float32 [1024, 256], P(('gx', 'gy')), may hold values from 0.1 to 1
- marker_owner: int32 [262144, 1], P(('gx', 'gy')), may hold values from 0 to 31; in each aligned block of 8192 rows (0 to 8191, 8192 to 16383, ...) at most 384 rows name the same one
- marker_element: int32 [262144], P(('gx', 'gy')), may hold values from 0 to 255
- marker_coords: float32 [3, 262144], P(None, ('gx', 'gy')), may hold values from -1 to 1
Outputs:
- new_positions: float32 [3, 1024, 256], P(None, ('gx', 'gy'))
- node_forces: float32 [3, 8192, 512], P(None, ('gx', 'gy'))
Inputs may be any that keep to these rules, and one draw needn't show every extreme that they name: `marker_owner`: among the markers of one device's rows, no owner is named more than 384 times, and in some devices' rows one owner is named exactly 384 times.
All inputs are finite; a program needn't handle non-finite values.
Results may differ from a plain program's by a relative error of at most 0.00013.
Values sent between devices are 32-bit elements; how exact they have to be, the bound alone decides.
No kernel may reach another device: no remote copies, remote signals or barrier semaphores. Data moves between devices by JAX's collectives and lax.ppermute only.
A program may use at most 64 MiB of HBM per device.

v0:
```python
import math
import jax
import jax.numpy as jnp
from jax import lax
from jax.sharding import PartitionSpec as P

POINTS = 8
bend_modulus = 0.05
time_step = 0.5


def padded(cells, sides, width):
    for axis, dim in sides:
        count = lax.axis_size(axis)
        head = lax.slice_in_dim(cells, 0, width, axis=dim)
        tail = lax.slice_in_dim(cells, cells.shape[dim] - width, cells.shape[dim], axis=dim)
        cells = jnp.concatenate(
            [
                lax.ppermute(tail, axis, [(i, (i + 1) % count) for i in range(count)]),
                cells,
                lax.ppermute(head, axis, [((i + 1) % count, i) for i in range(count)]),
            ],
            axis=dim,
        )
    return cells


def basis(values):
    abscissa = -jnp.cos(jnp.pi * jnp.arange(POINTS).astype(values.dtype) / (POINTS - 1))
    collected = []
    for i in range(POINTS):
        product = jnp.ones_like(values)
        for j in range(POINTS):
            if j != i:
                product = product * ((values - abscissa[j]) / (abscissa[i] - abscissa[j]))
        collected.append(product)
    return jnp.stack(collected)


def weight_table(factors):
    along_r = factors[0:POINTS].T
    along_s = factors[POINTS : 2 * POINTS].T
    along_t = factors[2 * POINTS : 3 * POINTS].T
    table = along_r[:, :, None, None] * along_s[:, None, :, None] * along_t[:, None, None, :]
    return table.reshape(along_r.shape[0], POINTS * POINTS * POINTS)


def surface_laplacian(extended):
    middle = extended[:, 1:-1]
    return (
        extended[:, 2:]
        + extended[:, :-2]
        + jnp.roll(middle, 1, axis=2)
        + jnp.roll(middle, -1, axis=2)
        - 4.0 * middle
    )


def tension(extended, stiff_h):
    points = extended[:3]
    vertical = extended[3]
    middle = points[:, 1:-1]
    return (
        stiff_h * (jnp.roll(middle, -1, axis=2) - middle)
        + jnp.roll(stiff_h, 1, axis=1) * (jnp.roll(middle, 1, axis=2) - middle)
        + vertical[1:-1] * (points[:, 2:] - middle)
        + vertical[:-2] * (points[:, :-2] - middle)
    )


def three_factors(coords):
    return jnp.concatenate([basis(coords[0]), basis(coords[1]), basis(coords[2])], axis=0)


def selector_of(block_elements, elem_count):
    return (block_elements[:, None] == jnp.arange(elem_count, dtype=jnp.int32)[None, :]).astype(
        jnp.float32
    )


def local(velocity, positions, stiff_h, stiff_v, marker_owner, marker_element, marker_coords):
    major_count = lax.axis_size("gx")
    minor_count = lax.axis_size("gy")
    devices_all = major_count * minor_count
    marker_count = marker_owner.shape[0]
    capacity = 3 * marker_count // (2 * devices_all)
    slot_total = devices_all * capacity
    elem_count = velocity.shape[1]
    stacked = jnp.concatenate([positions, stiff_v[None]], axis=0)
    extended = padded(stacked, ((("gx", "gy"), 1),), 1)
    pulling = tension(extended, stiff_h)
    laplace = surface_laplacian(extended[:3])
    laplace_wide = padded(laplace, ((("gx", "gy"), 1),), 1)
    bending = -bend_modulus * surface_laplacian(laplace_wide)
    marker_force = (pulling + bending).reshape(3, marker_count)
    owners = marker_owner[:, 0]
    ordering = jnp.argsort(owners, stable=True)
    sorted_owners = owners[ordering]
    offsets = jnp.searchsorted(sorted_owners, jnp.arange(devices_all, dtype=jnp.int32), side="left")
    within = jnp.arange(marker_count, dtype=jnp.int32) - offsets[sorted_owners]
    places = (
        jnp.zeros((marker_count,), jnp.int32).at[ordering].set(sorted_owners * capacity + within)
    )
    described = three_factors(marker_coords)
    lead = described.shape[0]
    payload = jnp.concatenate([described, marker_force], axis=0)
    width_all = payload.shape[0]
    outgoing = jnp.zeros((width_all, slot_total), jnp.float32).at[:, places].set(payload)
    slot_ids = jnp.zeros((1, slot_total), jnp.int32).at[:, places].set(marker_element[None])
    got_floats, got_slots = (
        lax.all_to_all(
            lax.all_to_all(
                outgoing.reshape(width_all, major_count, minor_count, capacity),
                "gx",
                split_axis=1,
                concat_axis=1,
                tiled=True,
            ),
            "gy",
            split_axis=2,
            concat_axis=2,
            tiled=True,
        ),
        lax.all_to_all(
            lax.all_to_all(
                slot_ids.reshape(1, major_count, minor_count, capacity),
                "gx",
                split_axis=1,
                concat_axis=1,
                tiled=True,
            ),
            "gy",
            split_axis=2,
            concat_axis=2,
            tiled=True,
        ),
    )
    got_floats = got_floats.reshape(width_all, slot_total)
    element_ids = got_slots.reshape(slot_total)
    factors = got_floats[:lead]
    pushes = got_floats[lead:]
    block_len = math.gcd(slot_total, 512)
    block_count = slot_total // block_len
    factor_blocks = factors.reshape(3 * POINTS, block_count, block_len).transpose(1, 0, 2)
    element_blocks = element_ids.reshape(block_count, block_len)
    push_blocks = pushes.reshape(3, block_count, block_len).transpose(1, 0, 2)

    def sample(inputs):
        block_factors, block_elements = inputs
        weights = weight_table(block_factors)
        selector = selector_of(block_elements, elem_count)
        gathered = jnp.einsum("be,ken->kbn", selector, velocity, precision=lax.Precision.HIGHEST)
        return jnp.sum(gathered * weights[None], axis=-1)

    sampled = lax.map(sample, (factor_blocks, element_blocks))
    returning = sampled.transpose(1, 0, 2).reshape(3, slot_total)
    arrived = lax.all_to_all(
        lax.all_to_all(
            returning.reshape(3, major_count, minor_count, capacity),
            "gx",
            split_axis=1,
            concat_axis=1,
            tiled=True,
        ),
        "gy",
        split_axis=2,
        concat_axis=2,
        tiled=True,
    )

    def deposit(running, inputs):
        block_factors, block_elements, block_pushes = inputs
        weights = weight_table(block_factors)
        selector = selector_of(block_elements, elem_count)
        loads = block_pushes[:, :, None] * weights[None]
        added = jnp.einsum("be,kbn->ken", selector, loads, precision=lax.Precision.HIGHEST)
        return (running + added, None)

    node_forces, unused = lax.scan(
        deposit, jnp.zeros_like(velocity), (factor_blocks, element_blocks, push_blocks)
    )
    moved = jnp.take(arrived.reshape(3, slot_total), places, axis=1).reshape(positions.shape)
    return (positions + time_step * moved, node_forces)


def solution(mesh):
    return jax.shard_map(
        local,
        mesh=mesh,
        in_specs=(
            P(None, ("gx", "gy"), None),
            P(None, ("gx", "gy"), None),
            P(("gx", "gy"), None),
            P(("gx", "gy"), None),
            P(("gx", "gy"), None),
            P(("gx", "gy")),
            P(None, ("gx", "gy")),
        ),
        out_specs=(P(None, ("gx", "gy"), None), P(None, ("gx", "gy"), None)),
        check_vma=False,
    )
```

profile of v0, /device:TPU:0, one launch (start us, length us, event | category | flops | bytes accessed | tf_op | source)
XLA Modules:
  0.0 586.4 jit_solution(10198000036078593590)
XLA Ops:
  2.0 6.0 %collective-permute-start = (f32[4,1,256]{2,1,0:T(1,128)S(1)}, f32[4,1,256]{2,1,0:T(1,128)S(1)}, u32[]{:S(2)}, u32[]{:S(2)}) collective-permute-start(f32[4,1,256]{2,1,0:T(1,128)S(1)} %get-tuple-element.267), channel_id=1, source_target_pairs={{1,0},{2,1},{3,2},{4,3},{5,4},{6,5},{7,6},{8,7},{9,8},{10,9},{11,1... | collective-permute-start | bytes 12296 | tf_op jit(solution)/shard_map/ppermute | solution.py:21
  8.0 7.5 %sort.17 = (s32[8192]{0:T(1024)}, s32[8192]{0:T(1024)S(1)}) sort(s32[8192]{0:T(1024)} %bitcast.127, s32[8192]{0:T(1024)S(1)} %iota.23), dimensions={0}, to_apply=%region_0.1 | sort | flops 106496 | bytes 131072 | tf_op jit(solution)/shard_map/jit(argsort)/sort | solution.py:97
  15.5 45.5 %gather_fusion.1 = s32[8192]{0:T(1024)S(1)} fusion(s32[8192]{0:T(1024)S(1)} %bitcast.128, s32[8192]{0:T(1024)S(1)} %get-tuple-element.305), kind=kCustom, calls=%fused_computation.1 | custom fusion | bytes 98304 | tf_op jit(solution)/shard_map/gather | solution.py:98
  61.1 10.5 %while.46 = (s32[]{:T(128)}, u32[32]{0:T(128)S(1)}, u32[32]{0:T(128)S(1)}, s32[8192]{0:T(1024)S(1)}, s32[]{:T(128)}, /*index=5*/s32[]{:T(128)}, s32[]{}) while((s32[]{:T(128)}, u32[32]{0:T(128)S(1)}, u32[32]{0:T(128)S(1)}, s32[8192]{0:T(1024)S(1)}, s32[]{:T(128)}, /*index=5*/s32[]{:T(128)}, s32[]{}) %tuple.172), condition=%wide.region_2.3_spmd.clone, body=%wide.region_1.2_spmd.clone.sunk | while | flops 1444 | bytes 5732 | solution.py:99
  80.0 15.9 %fusion.35 = s32[8192]{0:T(1024)S(1)} fusion(pred[8192]{0:T(1024)(128)(4,1)S(1)} %get-tuple-element.228, pred[8192]{0:T(1024)(128)(4,1)S(1)} %get-tuple-element.227, pred[8192]{0:T(1024)(128)(4,1)S(1)} %get-tuple-element.226, pred[8192]{0:T(1024)(128)(4,1)S(1)} %get-tuple-element.225, pred[8192]{0:T(1024)(128)(4,1)S(1)} %get-tuple-element.224, ...), kind=kLoop, calls=%fused_computation.250 | loop fusion | flops 229376 | bytes 303204 | tf_op jit(solution)/shard_map/add | solution.py:102
  95.9 30.5 %scatter_custom_fusion = s32[8192]{0:T(1024)S(1)} fusion(s32[8192]{0:T(1024)S(1)} %get-tuple-element.306, s32[8192]{0:T(1024)S(1)} %fusion.35, s32[]{:T(128)} %constant.79.clone.1), kind=kCustom, calls=%fused_computation.280 | custom fusion | bytes 32772 | tf_op jit(solution)/shard_map/scatter | solution.py:102
  126.4 30.7 %scatter_custom_fusion.1 = s32[12288]{0:T(1024)S(1)} fusion(s32[8192]{0:T(1024)S(1)} %get-tuple-element.304, s32[8192]{0:T(1024)} %param.18, s32[]{:T(128)} %constant.79.clone.1), kind=kCustom, calls=%fused_computation.252 | custom fusion | bytes 49664 | tf_op jit(solution)/shard_map/scatter | solution.py:109
  231.5 4.8 divide_multiply_fusion
  236.3 4.9 divide_multiply_fusion.6
  241.2 4.9 divide_multiply_fusion.12
  246.1 4.9 divide_multiply_fusion.18
  250.9 4.9 divide_multiply_fusion.24
  255.8 4.9 divide_multiply_fusion.30
  260.7 4.8 divide_multiply_fusion.36
  265.5 4.9 divide_multiply_fusion.42
  274.9 5.3 collective-permute-done.3
  284.4 23.9 %scatter_custom_fusion.2 = f32[27,12288]{0,1:T(8,128)} fusion(s32[8192]{0:T(1024)S(1)} %get-tuple-element.304, f32[8192,27]{1,0:T(8,128)} %copy.89, f32[]{:T(128)} %constant.87.clone.1), kind=kCustom, calls=%fused_computation.41 | custom fusion | bytes 1327616 | tf_op jit(solution)/shard_map/scatter | solution.py:108
  308.2 5.5 copy.90
  318.0 26.6 %all-to-all-done.2 = f32[27,8,4,384]{3,2,0,1:T(4,128)S(1)} async-done(((f32[27,8,4,384]{3,2,0,1:T(4,128)}), f32[27,8,4,384]{3,2,0,1:T(4,128)S(1)}, u32[]{:S(2)}, u32[]{:S(2)}) %all-to-all-start.2) | async-done | bytes 1327136 | tf_op jit(solution)/shard_map/all_to_all | solution.py:112
  357.5 16.7 %all-to-all-done.3 = f32[27,8,4,384]{3,1,0,2:T(8,128)} async-done(((f32[27,8,4,384]{3,1,0,2:T(8,128)}), f32[27,8,4,384]{3,1,0,2:T(8,128)}, u32[]{:S(2)}, u32[]{:S(2)}) %all-to-all-start.3) | async-done | bytes 1327136 | tf_op jit(solution)/shard_map/all_to_all | solution.py:111
  380.9 64.9 %while.45 = (s32[]{:T(128)}, f32[24,3,512]{2,1,0:T(4,128)S(1)}, s32[24,512]{1,0:T(8,128)S(1)}, f32[3,256,512]{1,2,0:T(8,128)S(1)}, f32[24,24,512]{2,1,0:T(8,128)}, /*index=5*/s32[]{:T(128)}, s32[]{:T(128)}, s32[]{}, s32[]{}) while((s32[]{:T(128)}, f32[24,3,512]{2,1,0:T(4,128)S(1)}, s32[24,512]{1,0:T(8,128)S(1)}, f32[3,256,512]{1,2,0:T(8,128)S(1)}, ...), condition=%wide.region_8.9_spmd, body=%wide.region_6.8_spmd.sunk | while | flops 2417916416 | bytes 4108425 | solution.py:155
  451.5 6.4 %all-to-all-done.4 = f32[3,8,4,384]{3,2,0,1:T(4,128)S(1)} async-done(((f32[3,8,4,384]{3,2,0,1:T(4,128)}), f32[3,8,4,384]{3,2,0,1:T(4,128)S(1)}, u32[]{:S(2)}, u32[]{:S(2)}) %all-to-all-start.4) | async-done | bytes 147488 | tf_op jit(solution)/shard_map/all_to_all | solution.py:158
  461.8 85.0 %while.47 = (s32[]{:T(128)}, f32[3,256,512]{1,2,0:T(8,128)S(1)}, f32[24,3,512]{2,0,1:T(8,128)S(1)}, f32[24,24,512]{2,1,0:T(8,128)}, s32[24,512]{1,0:T(8,128)S(1)}, /*index=5*/s32[]{:T(128)}, s32[]{:T(128)}, s32[]{}, s32[]{}) while((s32[]{:T(128)}, f32[3,256,512]{1,2,0:T(8,128)S(1)}, f32[24,3,512]{2,0,1:T(8,128)S(1)}, ...), condition=%wide.region_10.11_spmd.clone, body=%wide.region_9.10_spmd.clone.sunk | while | flops 2417917952 | bytes 5689491 | solution.py:179
  552.4 30.5 %gather_fusion.2 = f32[8192,3]{1,0:T(8,128)} fusion(f32[3,12288]{0,1:T(8,128)} %bitcast.133, s32[8192]{0:T(1024)S(1)} %get-tuple-element.303), kind=kCustom, calls=%fused_computation.2 | custom fusion | bytes 229376 | tf_op jit(solution)/shard_map/jit(_take)/gather | solution.py:182
  (446 shorter events, 223.5 us)
Async XLA Ops:
  0.6 14.9 %copy-start = (s32[8192,1]{0,1:T(1,128)S(1)}, s32[8192,1]{0,1:T(1,128)}, u32[]{:S(2)}) copy-start(s32[8192,1]{0,1:T(1,128)} %param.17) | copy-start | bytes 98308
  1.4 269.1 %collective-permute-start.1 = (f32[4,1,256]{2,1,0:T(1,128)S(1)}, f32[4,1,256]{2,1,0:T(1,128)S(1)}, u32[]{:S(2)}, u32[]{:S(2)}) collective-permute-start(f32[4,1,256]{2,1,0:T(1,128)S(1)} %get-tuple-element.268), channel_id=1, source_target_pairs={{0,1},{1,2},{2,3},{3,4},{4,5},{5,6},{6,7},{7,8},{8,9},{9,10},{10,1... | collective-permute-start | bytes 12296 | tf_op jit(solution)/shard_map/ppermute | solution.py:19
  2.0 268.6 %collective-permute-start = (f32[4,1,256]{2,1,0:T(1,128)S(1)}, f32[4,1,256]{2,1,0:T(1,128)S(1)}, u32[]{:S(2)}, u32[]{:S(2)}) collective-permute-start(f32[4,1,256]{2,1,0:T(1,128)S(1)} %get-tuple-element.267), channel_id=1, source_target_pairs={{1,0},{2,1},{3,2},{4,3},{5,4},{6,5},{7,6},{8,7},{9,8},{10,9},{11,1... | collective-permute-start | bytes 12296 | tf_op jit(solution)/shard_map/ppermute | solution.py:21
  61.0 170.1 %copy-start.1 = (f32[3,32,256]{2,1,0:T(8,128)S(1)}, f32[3,32,256]{2,1,0:T(8,128)}, u32[]{:S(2)}) copy-start(f32[3,32,256]{2,1,0:T(8,128)} %param.14) | copy-start | bytes 294916
  71.6 159.8 %copy-start.5 = (f32[32,256]{1,0:T(8,128)S(1)}, f32[32,256]{1,0:T(8,128)}, u32[]{:S(2)}) copy-start(f32[32,256]{1,0:T(8,128)} %param.15) | copy-start | bytes 98308
  71.6 159.8 %copy-start.2 = (f32[3,8192]{1,0:T(4,128)S(1)}, f32[3,8192]{1,0:T(4,128)}, u32[]{:S(2)}) copy-start(f32[3,8192]{1,0:T(4,128)} %param.19) | copy-start | bytes 294916
  80.0 190.5 %copy-start.4 = (f32[32,256]{1,0:T(8,128)S(1)}, f32[32,256]{1,0:T(8,128)}, u32[]{:S(2)}) copy-start(f32[32,256]{1,0:T(8,128)} %param.16) | copy-start | bytes 98308
  157.8 156.0 %all-to-all-start = ((s32[1,8,4,384]{3,2,0,1:T(4,128)}), s32[1,8,4,384]{3,2,0,1:T(4,128)S(1)}, u32[]{:S(2)}, u32[]{:S(2)}) async-start(s32[1,8,4,384]{3,2,0,1:T(4,128)} %reshape.123), calls=%async_computation | async-start | bytes 98304 | tf_op jit(solution)/shard_map/all_to_all | solution.py:125
  270.9 4.0 collective-permute-start.2
  273.5 6.6 %collective-permute-start.3 = (f32[3,1,256]{2,1,0:T(1,128)S(1)}, f32[3,1,256]{2,1,0:T(1,128)S(1)}, u32[]{:S(2)}, u32[]{:S(2)}) collective-permute-start(f32[3,1,256]{2,1,0:T(1,128)S(1)} %get-tuple-element.298), channel_id=1, source_target_pairs={{0,1},{1,2},{2,3},{3,4},{4,5},{5,6},{6,7},{7,8},{8,9},{9,10},{10,1... | collective-permute-start | bytes 9224 | tf_op jit(solution)/shard_map/ppermute | solution.py:19
  313.8 30.8 %all-to-all-start.2 = ((f32[27,8,4,384]{3,2,0,1:T(4,128)}), f32[27,8,4,384]{3,2,0,1:T(4,128)S(1)}, u32[]{:S(2)}, u32[]{:S(2)}) async-start(f32[27,8,4,384]{3,2,0,1:T(4,128)} %copy.90), calls=%async_computation.2 | async-start | bytes 2654208 | tf_op jit(solution)/shard_map/all_to_all | solution.py:112
  344.6 7.8 %all-to-all-start.1 = ((s32[1,8,4,384]{3,1,0,2:T(8,128)}), s32[1,8,4,384]{3,1,0,2:T(8,128)S(1)}, u32[]{:S(2)}, u32[]{:S(2)}) async-start(s32[1,8,4,384]{3,1,0,2:T(8,128)} %copy.87), calls=%async_computation.1 | async-start | bytes 98304 | tf_op jit(solution)/shard_map/all_to_all | solution.py:124
  349.5 7.4 %copy-start.3 = (f32[3,256,512]{2,1,0:T(8,128)S(1)}, f32[3,256,512]{2,1,0:T(8,128)}, u32[]{:S(2)}) copy-start(f32[3,256,512]{2,1,0:T(8,128)} %param.13) | copy-start | bytes 4718596
  352.4 21.8 %all-to-all-start.3 = ((f32[27,8,4,384]{3,1,0,2:T(8,128)}), f32[27,8,4,384]{3,1,0,2:T(8,128)}, u32[]{:S(2)}, u32[]{:S(2)}) async-start(f32[27,8,4,384]{3,1,0,2:T(8,128)} %copy.91), calls=%async_computation.3 | async-start | bytes 2654208 | tf_op jit(solution)/shard_map/all_to_all | solution.py:111
  446.6 11.2 %all-to-all-start.4 = ((f32[3,8,4,384]{3,2,0,1:T(4,128)}), f32[3,8,4,384]{3,2,0,1:T(4,128)S(1)}, u32[]{:S(2)}, u32[]{:S(2)}) async-start(f32[3,8,4,384]{3,2,0,1:T(4,128)} %copy.96), calls=%async_computation.4 | async-start | bytes 294912 | tf_op jit(solution)/shard_map/all_to_all | solution.py:158
  458.5 90.0 %all-to-all-start.5 = ((f32[3,8,4,384]{3,1,0,2:T(8,128)}), f32[3,8,4,384]{3,1,0,2:T(8,128)S(1)}, u32[]{:S(2)}, u32[]{:S(2)}) async-start(f32[3,8,4,384]{3,1,0,2:T(8,128)} %copy.97), calls=%async_computation.5 | async-start | bytes 294912 | tf_op jit(solution)/shard_map/all_to_all | solution.py:157
where the time goes:
time: 596 us; the launch traced here: 586 us
  local copies, waits for them, and re-layouts  242 us (41%)
  matrix products  103 us (17%)
  other arithmetic  78.1 us (13%)
  between operations  70.2 us (12%)
  waiting for transfers between devices  59.2 us (10%)
  starting transfers between devices  31.7 us (5%)
    dot_general x24, matrix products, deposit(): jnp.einsum('be,kbn->ken', selector, loads, precision=lax.Precision.HIGHEST)  60.9 us
    gather x1, local copies, waits for them, and re-layouts, local(): sorted_owners = owners[ordering]  45.5 us
    dot_general x24, matrix products, sample(): jnp.einsum('be,ken->kbn', selector, velocity, precision=lax.Precision.HIG...  41.8 us
    mul x8, other arithmetic, basis(): product = product * ((values - abscissa[j]) / (abscissa[i] - abscissa[j]))  39 us
    transpose x48, local copies, waits for them, and re-layouts, weight_table(): along_r = factors[0:POINTS].T  36.7 us
    gather x2, local copies, waits for them, and re-layouts, local(): jnp.take(arrived.reshape(3, slot_total), places, axis=1)  33.3 us
    scatter x1, local copies, waits for them, and re-layouts, local(): jnp.zeros((1, slot_total), jnp.int32).at[:, places]  30.7 us
    scatter x1, local copies, waits for them, and re-layouts, local(): jnp.zeros((marker_count,), jnp.int32).at[ordering]  30.5 us
  transfers between devices with their start and end apart: 10, of which 6 were waited for; matrix products, arithmetic and copies ran while one was open for 53% of the time, Pallas kernels for 0%

commit v1 on v0

--- a/solution.py
+++ b/solution.py
@@ -7,6 +7,30 @@
 POINTS = 8
 bend_modulus = 0.05
 time_step = 0.5
+
+
+def split_up(x, dim, peers):
+    lengths = x.shape
+    blocks = x.reshape(*lengths[:dim], peers, lengths[dim] // peers, *lengths[dim + 1 :])
+    return jnp.moveaxis(blocks, dim, 0)
+
+
+def in_order(pieces, dim):
+    dims = list(pieces.shape[1:])
+    dims[dim] *= pieces.shape[0]
+    return jnp.moveaxis(pieces, 0, dim).reshape(dims)
+
+
+def sent_to_each(value, axis, split_dim, concat_dim):
+    size, here = (lax.axis_size(axis), lax.axis_index(axis))
+    pieces = split_up(value, split_dim, size)
+    out = pieces
+    for step in range(1, size):
+        target, source = ((here + step) % size, (here - step) % size)
+        sent = lax.dynamic_index_in_dim(pieces, target, 0)
+        other = lax.ppermute(sent, axis, [(i, (i + step) % size) for i in range(size)])
+        out = lax.dynamic_update_slice_in_dim(out, other, source, axis=0)
+    return in_order(out, concat_dim)
 
 
 def padded(cells, sides, width):
@@ -108,7 +132,7 @@
     outgoing = jnp.zeros((width_all, slot_total), jnp.float32).at[:, places].set(payload)
     slot_ids = jnp.zeros((1, slot_total), jnp.int32).at[:, places].set(marker_element[None])
     got_floats, got_slots = (
-        lax.all_to_all(
+        sent_to_each(
             lax.all_to_all(
                 outgoing.reshape(width_all, major_count, minor_count, capacity),
                 "gx",
@@ -117,9 +141,8 @@
                 tiled=True,
             ),
             "gy",
-            split_axis=2,
-            concat_axis=2,
-            tiled=True,
+            2,
+            2,
         ),
         lax.all_to_all(
             lax.all_to_all(

time: 596 us -> 623 us (1.045)
  local copies, waits for them, and re-layouts: 242 us -> 280 us
  waiting for transfers between devices: 59.2 us -> 42.7 us
  blocking collectives: 0 us -> 10.8 us
  starting transfers between devices: 31.7 us -> 24.2 us
    dynamic_update_slice x0 -> x3, local copies, waits for them, and re-layouts: none -> 35.9 us  [sent_to_each(): out = lax.dynamic_update_slice_in_dim(out, other, source, axis=0)]
    all_to_all x2 -> x0, waiting for transfers between devices: 16.7 us -> none  [the longest x1 16.7 us: local(): lax.all_to_all(lax.all_to_all(outgoing.reshape(width_all, major_count, mi...]
    all_to_all x0 -> x1, blocking collectives: none -> 10.8 us  [local(): lax.all_to_all(slot_ids.reshape(1, major_count, minor_count, capacity), '...]
    all_to_all x2 -> x0, starting transfers between devices: 8.03 us -> none  [the longest x1 4.5 us: local(): lax.all_to_all(lax.all_to_all(outgoing.reshape(width_all, major_count, mi...]
  transfers between devices with their start and end apart: 10 -> 11, of which waited for: 6 -> 5; matrix products, arithmetic and copies ran while one was open for 53% -> 49% of each run, Pallas kernels for 0% -> 0%
where the time goes in v1:
time: 623 us; the launch traced here: 613 us
  local copies, waits for them, and re-layouts  280 us (45%)
  matrix products  103 us (17%)
  other arithmetic  78.4 us (13%)
  between operations  71 us (11%)
  waiting for transfers between devices  42.7 us (7%)
  starting transfers between devices  24.2 us (4%)
  blocking collectives  10.8 us (2%)
    dot_general x24, matrix products, deposit(): jnp.einsum('be,kbn->ken', selector, loads, precision=lax.Precision.HIGHEST)  60.9 us
    gather x1, local copies, waits for them, and re-layouts, local(): sorted_owners = owners[ordering]  45.5 us
    dot_general x24, matrix products, sample(): jnp.einsum('be,ken->kbn', selector, velocity, precision=lax.Precision.HIG...  41.8 us
    mul x8, other arithmetic, basis(): product = product * ((values - abscissa[j]) / (abscissa[i] - abscissa[j]))  39.2 us
    transpose x48, local copies, waits for them, and re-layouts, weight_table(): along_r = factors[0:POINTS].T  36.7 us
    dynamic_update_slice x3, local copies, waits for them, and re-layouts, sent_to_each(): out = lax.dynamic_update_slice_in_dim(out, other, source, axis=0)  35.9 us
    gather x2, local copies, waits for them, and re-layouts, local(): jnp.take(arrived.reshape(3, slot_total), places, axis=1)  33.3 us
    scatter x1, local copies, waits for them, and re-layouts, local(): jnp.zeros((1, slot_total), jnp.int32).at[:, places]  30.7 us
  transfers between devices with their start and end apart: 11, of which 5 were waited for; matrix products, arithmetic and copies ran while one was open for 49% of the time, Pallas kernels for 0%

profile of v1, /device:TPU:0, one launch (start us, length us, event | category | flops | bytes accessed | tf_op | source)
XLA Modules:
  0.0 613.0 jit_solution(13244898614364596956)
XLA Ops:
  2.0 6.0 collective-permute-start
  80.4 7.5 %sort.17 = (s32[8192]{0:T(1024)}, s32[8192]{0:T(1024)S(1)}) sort(s32[8192]{0:T(1024)} %bitcast.141, s32[8192]{0:T(1024)S(1)} %iota.23), dimensions={0}, to_apply=%region_0.1 | sort | flops 106496 | bytes 131072 | tf_op jit(solution)/shard_map/jit(argsort)/sort | solution.py:121
  88.0 45.5 %gather_fusion.1 = s32[8192]{0:T(1024)S(1)} fusion(s32[8192]{0:T(1024)S(1)} %bitcast.142, s32[8192]{0:T(1024)S(1)} %get-tuple-element.308), kind=kCustom, calls=%fused_computation.1 | custom fusion | bytes 98304 | tf_op jit(solution)/shard_map/gather | solution.py:122
  133.6 10.5 %while.46 = (s32[]{:T(128)}, u32[32]{0:T(128)S(1)}, u32[32]{0:T(128)S(1)}, s32[8192]{0:T(1024)S(1)}, s32[]{:T(128)}, /*index=5*/s32[]{:T(128)}, s32[]{}) while((s32[]{:T(128)}, u32[32]{0:T(128)S(1)}, u32[32]{0:T(128)S(1)}, s32[8192]{0:T(1024)S(1)}, s32[]{:T(128)}, /*index=5*/s32[]{:T(128)}, s32[]{}) %tuple.174), condition=%wide.region_2.3_spmd.clone, body=%wide.region_1.2_spmd.clone.sunk | while | flops 1444 | bytes 5732 | solution.py:123
  152.6 15.9 %fusion.35 = s32[8192]{0:T(1024)S(1)} fusion(pred[8192]{0:T(1024)(128)(4,1)S(1)} %get-tuple-element.228, pred[8192]{0:T(1024)(128)(4,1)S(1)} %get-tuple-element.227, pred[8192]{0:T(1024)(128)(4,1)S(1)} %get-tuple-element.226, pred[8192]{0:T(1024)(128)(4,1)S(1)} %get-tuple-element.225, pred[8192]{0:T(1024)(128)(4,1)S(1)} %get-tuple-element.224, ...), kind=kLoop, calls=%fused_computation.253 | loop fusion | flops 229376 | bytes 303204 | tf_op jit(solution)/shard_map/add | solution.py:126
  168.5 30.7 %scatter_custom_fusion = s32[8192]{0:T(1024)S(1)} fusion(s32[8192]{0:T(1024)S(1)} %get-tuple-element.309, s32[8192]{0:T(1024)S(1)} %fusion.35, s32[]{:T(128)} %constant.126.clone.1), kind=kCustom, calls=%fused_computation.283 | custom fusion | bytes 32772 | tf_op jit(solution)/shard_map/scatter | solution.py:126
  199.2 5.0 divide_multiply_fusion
  209.0 4.9 divide_multiply_fusion.12
  213.9 4.9 divide_multiply_fusion.18
  218.9 4.9 divide_multiply_fusion.24
  223.8 5.0 divide_multiply_fusion.30
  240.9 5.3 collective-permute-done.3
  250.4 23.9 %scatter_custom_fusion.2 = f32[27,12288]{0,1:T(8,128)} fusion(s32[8192]{0:T(1024)S(1)} %get-tuple-element.307, f32[8192,27]{1,0:T(8,128)} %copy.88, f32[]{:T(128)} %constant.134.clone.1), kind=kCustom, calls=%fused_computation.41 | custom fusion | bytes 1327616 | tf_op jit(solution)/shard_map/scatter | solution.py:132
  274.3 5.5 copy.89
  283.4 26.8 %all-to-all-done.2 = f32[27,8,4,384]{3,2,0,1:T(4,128)S(1)} async-done(((f32[27,8,4,384]{3,2,0,1:T(4,128)}), f32[27,8,4,384]{3,2,0,1:T(4,128)S(1)}, u32[]{:S(2)}, u32[]{:S(2)}) %all-to-all-start.2) | async-done | bytes 1327136 | tf_op jit(solution)/shard_map/all_to_all | solution.py:136
  315.4 30.7 %scatter_custom_fusion.1 = s32[12288]{0:T(1024)S(1)} fusion(s32[8192]{0:T(1024)S(1)} %get-tuple-element.307, s32[8192]{0:T(1024)} %param.18, s32[]{:T(128)} %constant.126.clone.1), kind=kCustom, calls=%fused_computation.255 | custom fusion | bytes 49664 | tf_op jit(solution)/shard_map/scatter | solution.py:133
  346.1 10.8 %all_to_all.25 = s32[1,8,4,384]{3,2,0,1:T(4,128)S(1)} all-to-all(s32[1,8,4,384]{3,2,0,1:T(4,128)S(1)} %reshape.134), channel_id=1, replica_groups=mesh['gx'=8,'gy'=4] {'gx'}, dimensions={1} | all-to-all | bytes 98304 | tf_op jit(solution)/shard_map/all_to_all | solution.py:148
  364.8 12.0 %dynamic_update_slice.13 = f32[4,27,8,1,384]{4,0,1,2,3:T(4,128)S(1)} dynamic-update-slice(f32[4,27,8,1,384]{4,0,1,2,3:T(4,128)S(1)} %bitcast.147, f32[1,27,8,1,384]{4,0,1,2,3:T(1,128)} %collective-permute-done.4, s32[]{:T(128)S(6)} %select_n.90, s32[]{:T(128)} %constant.126.clone.1, s32[]{:T(128)} %constant.126.clone.1, s32[]{:T(128)} %constant.126.clone.1, s32[]{:T(128)} %constant.126.clone.1) | dynamic-update-slice | bytes 663556 | tf_op jit(solution)/shard_map/dynamic_update_slice | solution.py:32
  376.8 12.0 %dynamic_update_slice.14 = f32[4,27,8,1,384]{4,0,1,2,3:T(4,128)S(1)} dynamic-update-slice(f32[4,27,8,1,384]{4,0,1,2,3:T(4,128)S(1)} %dynamic_update_slice.13, f32[1,27,8,1,384]{4,0,1,2,3:T(1,128)} %collective-permute-done.5, s32[]{:T(128)S(6)} %select_n.94, s32[]{:T(128)} %constant.126.clone.1, s32[]{:T(128)} %constant.126.clone.1, s32[]{:T(128)} %constant.126.clone.1, s32[]{:T(128)} %constant.126.clone.1) | dynamic-update-slice | bytes 663556 | tf_op jit(solution)/shard_map/dynamic_update_slice | solution.py:32
  388.7 12.0 %dynamic_update_slice.15 = f32[4,27,8,1,384]{4,0,1,2,3:T(4,128)S(1)} dynamic-update-slice(f32[4,27,8,1,384]{4,0,1,2,3:T(4,128)S(1)} %dynamic_update_slice.14, f32[1,27,8,1,384]{4,0,1,2,3:T(1,128)} %collective-permute-done.6, s32[]{:T(128)S(6)} %select_n.98, s32[]{:T(128)} %constant.126.clone.1, s32[]{:T(128)} %constant.126.clone.1, s32[]{:T(128)} %constant.126.clone.1, s32[]{:T(128)} %constant.126.clone.1) | dynamic-update-slice | bytes 663556 | tf_op jit(solution)/shard_map/dynamic_update_slice | solution.py:32
  408.1 64.9 %while.45 = (s32[]{:T(128)}, f32[24,3,512]{2,1,0:T(4,128)S(1)}, s32[24,512]{1,0:T(8,128)S(1)}, f32[3,256,512]{1,2,0:T(8,128)S(1)}, f32[24,24,512]{2,1,0:T(8,128)}, /*index=5*/s32[]{:T(128)}, s32[]{:T(128)}, s32[]{}, s32[]{}) while((s32[]{:T(128)}, f32[24,3,512]{2,1,0:T(4,128)S(1)}, s32[24,512]{1,0:T(8,128)S(1)}, f32[3,256,512]{1,2,0:T(8,128)S(1)}, ...), condition=%wide.region_8.9_spmd, body=%wide.region_6.8_spmd.sunk | while | flops 2417916416 | bytes 4108425 | solution.py:178
  477.3 7.2 %all-to-all-done.3 = f32[3,8,4,384]{3,2,0,1:T(4,128)S(1)} async-done(((f32[3,8,4,384]{3,2,0,1:T(4,128)}), f32[3,8,4,384]{3,2,0,1:T(4,128)S(1)}, u32[]{:S(2)}, u32[]{:S(2)}) %all-to-all-start.3) | async-done | bytes 147488 | tf_op jit(solution)/shard_map/all_to_all | solution.py:181
  488.5 84.9 %while.47 = (s32[]{:T(128)}, f32[3,256,512]{1,2,0:T(8,128)S(1)}, f32[24,3,512]{2,0,1:T(8,128)S(1)}, f32[24,24,512]{2,1,0:T(8,128)}, s32[24,512]{1,0:T(8,128)S(1)}, /*index=5*/s32[]{:T(128)}, s32[]{:T(128)}, s32[]{}, s32[]{}) while((s32[]{:T(128)}, f32[3,256,512]{1,2,0:T(8,128)S(1)}, f32[24,3,512]{2,0,1:T(8,128)S(1)}, ...), condition=%wide.region_10.11_spmd.clone, body=%wide.region_9.10_spmd.clone.sunk | while | flops 2417917952 | bytes 5689491 | solution.py:202
  579.0 30.5 %gather_fusion.2 = f32[8192,3]{1,0:T(8,128)} fusion(f32[3,12288]{0,1:T(8,128)} %bitcast.150, s32[8192]{0:T(1024)S(1)} %get-tuple-element.306), kind=kCustom, calls=%fused_computation.2 | custom fusion | bytes 229376 | tf_op jit(solution)/shard_map/jit(_take)/gather | solution.py:205
  (452 shorter events, 232.5 us)
Async XLA Ops:
  0.6 87.4 %copy-start = (s32[8192,1]{0,1:T(1,128)S(1)}, s32[8192,1]{0,1:T(1,128)}, u32[]{:S(2)}) copy-start(s32[8192,1]{0,1:T(1,128)} %param.17) | copy-start | bytes 98308
  1.4 237.1 %collective-permute-start.1 = (f32[4,1,256]{2,1,0:T(1,128)S(1)}, f32[4,1,256]{2,1,0:T(1,128)S(1)}, u32[]{:S(2)}, u32[]{:S(2)}) collective-permute-start(f32[4,1,256]{2,1,0:T(1,128)S(1)} %get-tuple-element.271), channel_id=1, source_target_pairs={{0,1},{1,2},{2,3},{3,4},{4,5},{5,6},{6,7},{7,8},{8,9},{9,10},{10,1... | collective-permute-start | bytes 12296 | tf_op jit(solution)/shard_map/ppermute | solution.py:43
  2.0 236.5 %collective-permute-start = (f32[4,1,256]{2,1,0:T(1,128)S(1)}, f32[4,1,256]{2,1,0:T(1,128)S(1)}, u32[]{:S(2)}, u32[]{:S(2)}) collective-permute-start(f32[4,1,256]{2,1,0:T(1,128)S(1)} %get-tuple-element.270), channel_id=1, source_target_pairs={{1,0},{2,1},{3,2},{4,3},{5,4},{6,5},{7,6},{8,7},{9,8},{10,9},{11,1... | collective-permute-start | bytes 12296 | tf_op jit(solution)/shard_map/ppermute | solution.py:45
  133.5 12.0 %copy-start.4 = (f32[32,256]{1,0:T(8,128)S(1)}, f32[32,256]{1,0:T(8,128)}, u32[]{:S(2)}) copy-start(f32[32,256]{1,0:T(8,128)} %param.15) | copy-start | bytes 98308
  133.5 65.6 %copy-start.2 = (f32[3,8192]{1,0:T(4,128)S(1)}, f32[3,8192]{1,0:T(4,128)}, u32[]{:S(2)}) copy-start(f32[3,8192]{1,0:T(4,128)} %param.19) | copy-start | bytes 294916
  144.1 94.4 %copy-start.1 = (f32[3,32,256]{2,1,0:T(8,128)S(1)}, f32[3,32,256]{2,1,0:T(8,128)}, u32[]{:S(2)}) copy-start(f32[3,32,256]{2,1,0:T(8,128)} %param.14) | copy-start | bytes 294916
  144.1 94.4 %copy-start.3 = (f32[32,256]{1,0:T(8,128)S(1)}, f32[32,256]{1,0:T(8,128)}, u32[]{:S(2)}) copy-start(f32[32,256]{1,0:T(8,128)} %param.16) | copy-start | bytes 98308
  238.8 2.0 collective-permute-start.2
  239.6 6.6 %collective-permute-start.3 = (f32[3,1,256]{2,1,0:T(1,128)S(1)}, f32[3,1,256]{2,1,0:T(1,128)S(1)}, u32[]{:S(2)}, u32[]{:S(2)}) collective-permute-start(f32[3,1,256]{2,1,0:T(1,128)S(1)} %get-tuple-element.301), channel_id=1, source_target_pairs={{0,1},{1,2},{2,3},{3,4},{4,5},{5,6},{6,7},{7,8},{8,9},{9,10},{10,1... | collective-permute-start | bytes 9224 | tf_op jit(solution)/shard_map/ppermute | solution.py:43
  279.8 30.4 %all-to-all-start.2 = ((f32[27,8,4,384]{3,2,0,1:T(4,128)}), f32[27,8,4,384]{3,2,0,1:T(4,128)S(1)}, u32[]{:S(2)}, u32[]{:S(2)}) async-start(f32[27,8,4,384]{3,2,0,1:T(4,128)} %copy.89), calls=%async_computation.2 | async-start | bytes 2654208 | tf_op jit(solution)/shard_map/all_to_all | solution.py:136
  311.9 52.8 %collective-permute-start.4 = (f32[1,27,8,1,384]{4,0,1,2,3:T(1,128)}, f32[1,27,8,1,384]{4,0,1,2,3:T(1,128)}, u32[]{:S(2)}, u32[]{:S(2)}) collective-permute-start(f32[1,27,8,1,384]{4,0,1,2,3:T(1,128)} %get-tuple-element.269), channel_id=1, source_target_pairs={{0,1},{1,2},{2,3},{3,0},{4,5},{5,6},{6,7},{7,4},{8,9},{9,10},{10,1... | collective-permute-start | bytes 995336 | tf_op jit(solution)/shard_map/ppermute | solution.py:31
  311.9 64.8 %collective-permute-start.5 = (f32[1,27,8,1,384]{4,0,1,2,3:T(1,128)}, f32[1,27,8,1,384]{4,0,1,2,3:T(1,128)}, u32[]{:S(2)}, u32[]{:S(2)}) collective-permute-start(f32[1,27,8,1,384]{4,0,1,2,3:T(1,128)} %get-tuple-element.268), channel_id=1, source_target_pairs={{0,2},{1,3},{2,0},{3,1},{4,6},{5,7},{6,4},{7,5},{8,10},{9,11},{10,... | collective-permute-start | bytes 995336 | tf_op jit(solution)/shard_map/ppermute | solution.py:31
  314.8 73.9 %collective-permute-start.6 = (f32[1,27,8,1,384]{4,0,1,2,3:T(1,128)S(1)}, f32[1,27,8,1,384]{4,0,1,2,3:T(1,128)}, u32[]{:S(2)}, u32[]{:S(2)}) collective-permute-start(f32[1,27,8,1,384]{4,0,1,2,3:T(1,128)S(1)} %get-tuple-element.267), channel_id=1, source_target_pairs={{0,3},{1,0},{2,1},{3,2},{4,7},{5,4},{6,5},{7,6},{8,11},{9,8},{10,9... | collective-permute-start | bytes 995336 | tf_op jit(solution)/shard_map/ppermute | solution.py:31
  357.4 7.3 %all-to-all-start.1 = ((s32[1,8,4,384]{3,1,0,2:T(8,128)}), s32[1,8,4,384]{3,1,0,2:T(8,128)S(1)}, u32[]{:S(2)}, u32[]{:S(2)}) async-start(s32[1,8,4,384]{3,1,0,2:T(8,128)} %copy.86), calls=%async_computation.1 | async-start | bytes 98304 | tf_op jit(solution)/shard_map/all_to_all | solution.py:147
  405.1 3.0 copy-start.5
  473.7 10.8 %all-to-all-start.3 = ((f32[3,8,4,384]{3,2,0,1:T(4,128)}), f32[3,8,4,384]{3,2,0,1:T(4,128)S(1)}, u32[]{:S(2)}, u32[]{:S(2)}) async-start(f32[3,8,4,384]{3,2,0,1:T(4,128)} %copy.94), calls=%async_computation.3 | async-start | bytes 294912 | tf_op jit(solution)/shard_map/all_to_all | solution.py:181
  485.2 89.9 %all-to-all-start.4 = ((f32[3,8,4,384]{3,1,0,2:T(8,128)}), f32[3,8,4,384]{3,1,0,2:T(8,128)S(1)}, u32[]{:S(2)}, u32[]{:S(2)}) async-start(f32[3,8,4,384]{3,1,0,2:T(8,128)} %copy.95), calls=%async_computation.4 | async-start | bytes 294912 | tf_op jit(solution)/shard_map/all_to_all | solution.py:180
